TPU v7x, 32 devices: a whole 2x2x4 slice. The times are simulated.
32 devices in a mesh: dp: 2 (over x), ctx: 4 (over y, core), tp: 4 (over z).
Axes of the slice: x: 2, y: 2, z: 4, core: 2. Of those that a mesh axis runs over, the one named last changes fastest.
Arguments:
- block_input: bfloat16 [2, 8, 256, 2048], P('dp', 'ctx', 'tp'), may hold values from -6 to 6
- block_order: int32 [2, 8], P('dp'), may hold values from 0 to 7, each once within a row
- w_qkv: bfloat16 [2048, 3, 2048], P(('dp', 'ctx'), None, 'tp'), may hold values from -1 to 1
- w_out: bfloat16 [2048, 2048], P('tp', ('dp', 'ctx')), may hold values from -3 to 3
- gain_attn: bfloat16 [2048], P(('dp', 'ctx')), may hold values from 0.5 to 1.5
- w_gate_up: bfloat16 [2048, 2, 8192], P(('dp', 'ctx'), None, 'tp'), may hold values from -0.125 to 0.125
- w_down: bfloat16 [8192, 2048], P('tp', ('dp', 'ctx')), may hold values from -0.0625 to 0.0625
- gain_mlp: bfloat16 [2048], P(('dp', 'ctx')), may hold values from 0.5 to 1.5
- cotangent: bfloat16 [2, 8, 256, 2048], P('dp', 'ctx', 'tp'), may hold values from -6 to 6
Outputs:
- block_output: bfloat16 [2, 8, 256, 2048], P('dp', 'ctx', 'tp')
- input_grad: float32 [2, 8, 256, 2048], P('dp', 'ctx', 'tp')
- grad_qkv: float32 [2048, 3, 2048], P(('dp', 'ctx'), None, 'tp')
- grad_out: float32 [2048, 2048], P('tp', ('dp', 'ctx'))
- grad_gain_attn: float32 [2048], P(('dp', 'ctx'))
- grad_gate_up: float32 [2048, 2, 8192], P(('dp', 'ctx'), None, 'tp')
- grad_down: float32 [8192, 2048], P('tp', ('dp', 'ctx'))
- grad_gain_mlp: float32 [2048], P(('dp', 'ctx'))
Inputs may be any that keep to these rules, and one draw needn't show every extreme that they name: `block_order`: each row lists every block number of one sequence once.
All inputs are finite; a program needn't handle non-finite values.
Results may differ from a plain program's by a relative error of at most 0.019.
Values may be sent and summed in bfloat16 or wider, within the bound.
A program may use at most 192 MiB of HBM per device.

v0:
```python
import jax
import jax.numpy as jnp
from jax import lax
from jax.sharding import PartitionSpec as P

HEAD_DIM = 64
EPSILON = 1e-05
ROPE_BASE = 130000.0
NEG_LARGE = -1e30


def rope_tables(positions, head_size):
    half = head_size // 2
    freq = ROPE_BASE ** (-(jnp.arange(half, dtype=jnp.float32) * 2.0 / head_size))
    angle = positions.astype(jnp.float32)[..., None] * freq
    cosine = jnp.cos(angle)
    sine = jnp.sin(angle)
    return (jnp.concatenate([cosine, cosine], -1), jnp.concatenate([sine, sine], -1))


def rotate(values):
    half = values.shape[-1] // 2
    return jnp.concatenate([-values[..., half:], values[..., :half]], -1)


def unrotate(values):
    half = values.shape[-1] // 2
    return jnp.concatenate([values[..., half:], -values[..., :half]], -1)


def rope_apply(values, cosine, sine):
    return values * cosine + rotate(values) * sine


def rope_back(grads, cosine, sine):
    return grads * cosine + unrotate(grads * sine)


def gather_rows(values):
    return lax.all_gather(values, "tp", axis=2, tiled=True)


def sum_rows(values):
    return lax.psum_scatter(values, "tp", scatter_dimension=2, tiled=True)


def gather_cotangent(values):
    return lax.all_gather(values, "tp", axis=2, tiled=True)


def sum_normed(values):
    return lax.psum_scatter(values, "tp", scatter_dimension=2, tiled=True)


def block_scores(query, key_blk, query_pos, key_pos, head_count):
    key_heads = key_blk.reshape(key_blk.shape[0], head_count, HEAD_DIM)
    scores = jnp.einsum("qhe,khe->hqk", query, key_heads, preferred_element_type=jnp.float32)
    visible = key_pos[None, :] <= query_pos[:, None]
    return jnp.where(visible[None], scores, -jnp.inf)


def online_update(state, query, query_pos, key_blk, value_blk, key_pos, head_count):
    run_max, run_sum, run_acc = state
    scores = block_scores(query, key_blk, query_pos, key_pos, head_count)
    new_max = jnp.maximum(run_max, jnp.max(scores, -1))
    factor = jnp.exp(run_max - new_max)
    probs = jnp.exp(scores - new_max[..., None])
    new_sum = run_sum * factor + jnp.sum(probs, -1)
    value_heads = value_blk.reshape(value_blk.shape[0], head_count, HEAD_DIM).astype(jnp.float32)
    mixed = jnp.einsum("hqk,khe->qhe", probs, value_heads, precision=lax.Precision.HIGHEST)
    new_acc = run_acc * factor.T[:, :, None] + mixed
    return (new_max, new_sum, new_acc)


def backward_block(
    query, query_pos, grad_blk, log_total, delta, key_blk, value_blk, key_pos, head_count
):
    scores = block_scores(query, key_blk, query_pos, key_pos, head_count)
    probs = jnp.exp(scores - log_total[..., None])
    value_heads = value_blk.reshape(value_blk.shape[0], head_count, HEAD_DIM)
    key_heads = key_blk.reshape(key_blk.shape[0], head_count, HEAD_DIM)
    dprobs = jnp.einsum("qhe,khe->hqk", grad_blk, value_heads, preferred_element_type=jnp.float32)
    grad_scores = (probs * (dprobs - delta[..., None])).astype(jnp.bfloat16)
    grad_query = jnp.einsum(
        "hqk,khe->qhe", grad_scores, key_heads, preferred_element_type=jnp.float32
    )
    grad_key = jnp.einsum("hqk,qhe->khe", grad_scores, query, preferred_element_type=jnp.float32)
    grad_value = jnp.einsum(
        "hqk,qhe->khe", probs.astype(jnp.bfloat16), grad_blk, preferred_element_type=jnp.float32
    )
    flat_width = head_count * HEAD_DIM
    return (grad_query, grad_key.reshape(-1, flat_width), grad_value.reshape(-1, flat_width))


def body(block_input, block_order, w_qkv, w_out, gain_attn, w_gate_up, w_down, gain_mlp, cotangent):
    f32 = jnp.float32
    bf16 = jnp.bfloat16
    seq_count = block_input.shape[0]
    row_count = block_input.shape[2]
    span = row_count * lax.axis_size("tp")
    local_width = w_qkv.shape[2]
    head_count = local_width // HEAD_DIM
    query_rows = 2 * span
    block_total = block_order.shape[1]
    ctx_index = lax.axis_index("ctx")
    my_ids = lax.dynamic_slice_in_dim(block_order, ctx_index * 2, 2, 1)
    offsets = jnp.arange(span, dtype=jnp.int32)
    query_pos = (my_ids[:, :, None] * span + offsets).reshape(seq_count, query_rows)
    cosine, sine = rope_tables(query_pos, HEAD_DIM)
    cosine = cosine[:, :, None, :]
    sine = sine[:, :, None, :]
    full_qkv, full_out, full_gain_attn = (
        lax.all_gather(w_qkv, ("dp", "ctx"), axis=0, tiled=True),
        lax.all_gather(w_out, ("dp", "ctx"), axis=1, tiled=True),
        lax.all_gather(gain_attn, ("dp", "ctx"), axis=0, tiled=True),
    )
    x_float = block_input.astype(f32)
    rms_attn = lax.rsqrt(jnp.mean(x_float * x_float, -1, keepdims=True) + EPSILON)
    unit_attn = x_float * rms_attn
    normed_attn = (unit_attn * full_gain_attn.astype(f32)).astype(bf16)
    normed_attn_full = gather_rows(normed_attn)
    qkv = jnp.einsum("spcd,dte->spcte", normed_attn_full, full_qkv, preferred_element_type=f32)
    qkv = qkv.reshape(seq_count, query_rows, 3, head_count, HEAD_DIM)
    queries = (rope_apply(qkv[:, :, 0], cosine, sine) * 0.125).astype(bf16)
    keys = rope_apply(qkv[:, :, 1], cosine, sine).astype(bf16)
    values = qkv[:, :, 2].astype(bf16)
    key_send = keys.reshape(seq_count, 2, span, local_width)
    value_send = values.reshape(seq_count, 2, span, local_width)
    initial = (
        jnp.full((seq_count, head_count, query_rows), NEG_LARGE, f32),
        jnp.zeros((seq_count, head_count, query_rows), f32),
        jnp.zeros((seq_count, query_rows, head_count, HEAD_DIM), f32),
    )
    key_piece = lax.all_gather(key_send, "ctx", axis=1, tiled=True)
    value_piece = lax.all_gather(value_send, "ctx", axis=1, tiled=True)

    def visit(step_index, inner):
        run_max, run_sum, run_acc = inner
        key_ids = lax.dynamic_index_in_dim(block_order, step_index, 1, False)
        key_blk = lax.dynamic_index_in_dim(key_piece, step_index, 1, False)
        value_blk = lax.dynamic_index_in_dim(value_piece, step_index, 1, False)
        member = 0
        key_pos = key_ids[member] * span + offsets
        operands = (run_max[member], run_sum[member], run_acc[member])

        def update(current, member=member, key_pos=key_pos):
            return online_update(
                current,
                queries[member],
                query_pos[member],
                key_blk[member],
                value_blk[member],
                key_pos,
                head_count,
            )

        result = update(operands)
        maxes = [result[0]]
        sums = [result[1]]
        accs = [result[2]]
        return (jnp.stack(maxes), jnp.stack(sums), jnp.stack(accs))

    run_max, run_sum, run_acc = lax.fori_loop(0, key_piece.shape[1], visit, initial)
    attention = (run_acc / jnp.transpose(run_sum, (0, 2, 1))[..., None]).astype(bf16)
    log_total = run_max + jnp.log(run_sum)
    attn_flat = attention.reshape(seq_count, 2, span, local_width)
    attn_part = jnp.einsum("spce,ed->spcd", attn_flat, full_out, preferred_element_type=f32)
    resid_mid = x_float + sum_rows(attn_part)
    full_gate_up, full_down, full_gain_mlp = (
        lax.all_gather(w_gate_up, ("dp", "ctx"), axis=0, tiled=True),
        lax.all_gather(w_down, ("dp", "ctx"), axis=1, tiled=True),
        lax.all_gather(gain_mlp, ("dp", "ctx"), axis=0, tiled=True),
    )
    rms_mlp = lax.rsqrt(jnp.mean(resid_mid * resid_mid, -1, keepdims=True) + EPSILON)
    unit_mlp = resid_mid * rms_mlp
    normed_mlp = (unit_mlp * full_gain_mlp.astype(f32)).astype(bf16)
    normed_mlp_full = gather_rows(normed_mlp)
    gate_up = jnp.einsum(
        "spcd,dtf->spctf", normed_mlp_full, full_gate_up, preferred_element_type=f32
    )
    gate = gate_up[:, :, :, 0]
    upper = gate_up[:, :, :, 1]
    sigma = jax.nn.sigmoid(gate)
    hidden = (gate * sigma * upper).astype(bf16)
    down_part = jnp.einsum("spcf,fd->spcd", hidden, full_down, preferred_element_type=f32)
    resid_out = resid_mid + sum_rows(down_part)
    block_output = resid_out.astype(bf16)
    back_gate_up, back_down, back_gain_mlp = (full_gate_up, full_down, full_gain_mlp)
    back_qkv, back_out, back_gain_attn = (full_qkv, full_out, full_gain_attn)
    cotan_full = gather_cotangent(cotangent)
    grad_down_local = jnp.einsum("spcf,spcd->fd", hidden, cotan_full, preferred_element_type=f32)
    grad_hidden = jnp.einsum("spcd,fd->spcf", cotan_full, back_down, preferred_element_type=f32)
    act_grad = jnp.stack(
        [grad_hidden * upper * sigma * (1.0 + gate * (1.0 - sigma)), grad_hidden * gate * sigma],
        axis=3,
    ).astype(bf16)
    grad_gate_up_local = jnp.einsum(
        "spcd,spctf->dtf", normed_mlp_full, act_grad, preferred_element_type=f32
    )
    grad_normed_mlp = sum_normed(
        jnp.einsum("spctf,dtf->spcd", act_grad, back_gate_up, preferred_element_type=f32)
    )
    gain_term_mlp = jnp.sum(grad_normed_mlp * unit_mlp, axis=(0, 1, 2))
    scaled_two = grad_normed_mlp * back_gain_mlp.astype(f32)
    grad_mid = cotangent.astype(f32) + rms_mlp * (
        scaled_two - unit_mlp * jnp.mean(scaled_two * unit_mlp, -1, keepdims=True)
    )
    mlp_shares = (
        lax.psum_scatter(
            grad_gate_up_local.astype(jnp.bfloat16), ("dp", "ctx"), scatter_dimension=0, tiled=True
        ).astype(jnp.float32),
        lax.psum_scatter(
            grad_down_local.astype(jnp.bfloat16), ("dp", "ctx"), scatter_dimension=1, tiled=True
        ).astype(jnp.float32),
        lax.psum_scatter(
            gain_term_mlp.astype(jnp.bfloat16), ("dp", "ctx"), scatter_dimension=0, tiled=True
        ).astype(jnp.float32),
    )
    grad_mid_b = grad_mid.astype(bf16)
    mid_full = gather_cotangent(grad_mid_b)
    grad_out_local = jnp.einsum("spce,spcd->ed", attn_flat, mid_full, preferred_element_type=f32)
    grad_attention = jnp.einsum(
        "spcd,ed->spce", mid_full, back_out, preferred_element_type=f32
    ).astype(bf16)
    grad_attention = grad_attention.reshape(seq_count, query_rows, head_count, HEAD_DIM)
    delta = jnp.transpose(
        jnp.sum(grad_attention.astype(f32) * attention.astype(f32), -1), (0, 2, 1)
    )
    all_keys, all_values = (
        lax.all_gather(key_send, "ctx", axis=1, tiled=True),
        lax.all_gather(value_send, "ctx", axis=1, tiled=True),
    )

    def back_step(grad_queries, slot):
        key_ids = lax.dynamic_index_in_dim(block_order, slot, 1, False)
        key_blk = lax.dynamic_index_in_dim(all_keys, slot, 1, False)
        value_blk = lax.dynamic_index_in_dim(all_values, slot, 1, False)
        member = 0
        key_pos = key_ids[member] * span + offsets

        def work(current, member=member, key_pos=key_pos):
            grad_query, grad_key, grad_value = backward_block(
                queries[member],
                query_pos[member],
                grad_attention[member],
                log_total[member],
                delta[member],
                key_blk[member],
                value_blk[member],
                key_pos,
                head_count,
            )
            return (current + grad_query, grad_key, grad_value)

        result = work(grad_queries[member])
        query_list = [result[0]]
        key_list = [result[1]]
        value_list = [result[2]]
        return (jnp.stack(query_list), (jnp.stack(key_list), jnp.stack(value_list)))

    start_grads = jnp.zeros((seq_count, query_rows, head_count, HEAD_DIM), f32)
    grad_queries, (key_terms, value_terms) = lax.scan(
        back_step, start_grads, jnp.arange(block_total, dtype=jnp.int32)
    )
    grad_keys, grad_values = (
        lax.psum_scatter(
            key_terms.astype(jnp.bfloat16), "ctx", scatter_dimension=0, tiled=True
        ).astype(jnp.float32),
        lax.psum_scatter(
            value_terms.astype(jnp.bfloat16), "ctx", scatter_dimension=0, tiled=True
        ).astype(jnp.float32),
    )
    grad_keys = jnp.transpose(grad_keys, (1, 0, 2, 3)).reshape(
        seq_count, query_rows, head_count, HEAD_DIM
    )
    grad_values = jnp.transpose(grad_values, (1, 0, 2, 3)).reshape(
        seq_count, query_rows, head_count, HEAD_DIM
    )
    qkv_grad = jnp.stack(
        [
            rope_back(grad_queries, cosine, sine) * 0.125,
            rope_back(grad_keys, cosine, sine),
            grad_values,
        ],
        axis=2,
    ).astype(bf16)
    qkv_grad = qkv_grad.reshape(seq_count, 2, span, 3, local_width)
    grad_qkv_local = jnp.einsum(
        "spcd,spcte->dte", normed_attn_full, qkv_grad, preferred_element_type=f32
    )
    grad_normed_attn = sum_normed(
        jnp.einsum("spcte,dte->spcd", qkv_grad, back_qkv, preferred_element_type=f32)
    )
    gain_term_attn = jnp.sum(grad_normed_attn * unit_attn, axis=(0, 1, 2))
    scaled_one = grad_normed_attn * back_gain_attn.astype(f32)
    input_grad = grad_mid + rms_attn * (
        scaled_one - unit_attn * jnp.mean(scaled_one * unit_attn, -1, keepdims=True)
    )
    shard_qkv, shard_out, shard_gain_attn = (
        lax.psum_scatter(
            grad_qkv_local.astype(jnp.bfloat16), ("dp", "ctx"), scatter_dimension=0, tiled=True
        ).astype(jnp.float32),
        lax.psum_scatter(
            grad_out_local.astype(jnp.bfloat16), ("dp", "ctx"), scatter_dimension=1, tiled=True
        ).astype(jnp.float32),
        lax.psum_scatter(
            gain_term_attn.astype(jnp.bfloat16), ("dp", "ctx"), scatter_dimension=0, tiled=True
        ).astype(jnp.float32),
    )
    shard_gate_up, shard_down, shard_gain_mlp = mlp_shares
    total_gain_attn, total_gain_mlp = lax.psum((shard_gain_attn, shard_gain_mlp), "tp")
    return (
        block_output,
        input_grad,
        shard_qkv,
        shard_out,
        total_gain_attn,
        shard_gate_up,
        shard_down,
        total_gain_mlp,
    )


def solution(mesh):
    in_specs = (
        P("dp", "ctx", "tp", None),
        P("dp", None),
        P(("dp", "ctx"), None, "tp"),
        P("tp", ("dp", "ctx")),
        P(("dp", "ctx")),
        P(("dp", "ctx"), None, "tp"),
        P("tp", ("dp", "ctx")),
        P(("dp", "ctx")),
        P("dp", "ctx", "tp", None),
    )
    out_specs = (
        P("dp", "ctx", "tp", None),
        P("dp", "ctx", "tp", None),
        P(("dp", "ctx"), None, "tp"),
        P("tp", ("dp", "ctx")),
        P(("dp", "ctx")),
        P(("dp", "ctx"), None, "tp"),
        P("tp", ("dp", "ctx")),
        P(("dp", "ctx")),
    )
    return jax.shard_map(body, mesh=mesh, in_specs=in_specs, out_specs=out_specs, check_vma=False)
```

profile of v0, /device:TPU:0, one launch (start us, length us, event | category | flops | bytes accessed | tf_op | source)
XLA Modules:
  0.0 1424.0 jit_solution(8658560242486038990)
XLA Ops:
  8.6 10.4 all-gather
  27.8 30.2 %all-gather.15.cloned.1.call-done = bf16[2048,3,512]{2,0,1:T(8,128)(2,1)} async-done(((bf16[256,3,512]{2,0,1:T(8,128)(2,1)}), bf16[2048,3,512]{2,0,1:T(8,128)(2,1)}) %all-gather.15.cloned.1.call-update) | async-done | bytes 6291472 | tf_op jit(solution)/shard_map/all_gather | solution.py:113
  58.0 8.8 copy.74
  66.9 39.0 %all-gather.13.cloned.1.call-done = bf16[1,2,256,2048]{3,2,1,0:T(8,128)(2,1)} async-done(((bf16[1,2,64,2048]{3,2,1,0:T(8,128)(2,1)}), bf16[1,2,256,2048]{3,2,1,0:T(8,128)(2,1)}) %all-gather.13.cloned.1.call-update) | async-done | bytes 2097168 | tf_op jit(solution)/shard_map/all_gather | solution.py:40
  105.9 6.2 convolution_bitcast_fusion.2
  115.9 2.8 concatenate.55
  118.7 2.8 squeeze.94
  121.6 3.9 add_convert_fusion.1
  133.6 15.4 %all-gather.17.cloned.1.call-done = bf16[1,8,256,512]{3,2,0,1:T(8,128)(2,1)} async-done(((bf16[1,2,256,512]{3,2,0,1:T(8,128)(2,1)}), bf16[1,8,256,512]{3,2,0,1:T(8,128)(2,1)}) %all-gather.17.cloned.1.call-update) | async-done | bytes 2097168 | tf_op jit(solution)/shard_map/all_gather | solution.py:134
  149.0 3.9 copy.77
  152.9 20.7 %all-gather.19.cloned.1.call-done = bf16[1,8,256,512]{3,2,0,1:T(8,128)(2,1)} async-done(((bf16[1,2,256,512]{3,2,0,1:T(8,128)(2,1)}), bf16[1,8,256,512]{3,2,0,1:T(8,128)(2,1)}) %all-gather.19.cloned.1.call-update) | async-done | bytes 2097168 | tf_op jit(solution)/shard_map/all_gather | solution.py:135
  173.6 3.9 copy.78
  177.6 92.5 %while.34 = (s32[]{:T(128)}, f32[1,8,512]{2,1,0:T(8,128)S(1)}, f32[1,8,512]{2,1,0:T(8,128)S(1)}, f32[1,512,8,64]{1,3,2,0:T(8,128)S(1)}, s32[1,8]{1,0:T(1,128)S(1...) while((s32[]{:T(128)}, f32[1,8,512]{2,1,0:T(8,128)S(1)}, ...), condition=%wide.region_4.5_spmd.clone, body=%wide.region_1.4_spmd.clone.sunk | while | flops 947548928 | bytes 34334904 | solution.py:163
  180.2 2.8 fusion.165
  183.0 3.1 fusion.167
  186.5 2.7 fusion.168
  191.8 2.8 fusion.165
  194.6 3.1 fusion.167
  198.0 2.7 fusion.168
  203.3 2.8 fusion.165
  206.1 3.1 fusion.167
  214.9 2.8 fusion.165
  217.7 3.1 fusion.167
  226.4 2.8 fusion.165
  229.3 3.1 fusion.167
  238.0 2.8 fusion.165
  240.8 3.1 fusion.167
  249.5 2.8 fusion.165
  252.4 3.1 fusion.167
  261.1 2.8 fusion.165
  263.9 3.1 fusion.167
  270.4 5.1 convolution_bitcast_fusion.1
  276.1 8.9 all-gather.1
  285.1 67.6 %reduce-scatter.11.cloned.1.call-done = f32[1,2,64,2048]{3,2,1,0:T(8,128)} async-done(((f32[1,2,256,2048]{3,2,1,0:T(8,128)}), f32[1,2,64,2048]{3,2,1,0:T(8,128)}) %reduce-scatter.11.cloned.1.call-update) | async-done | bytes 1048592 | tf_op jit(solution)/shard_map/reduce_scatter | solution.py:44
  355.4 3.8 copy.80
  361.0 40.7 %all-gather.23.cloned.1.call-done = bf16[1,2,256,2048]{3,2,1,0:T(8,128)(2,1)} async-done(((bf16[1,2,64,2048]{3,2,1,0:T(8,128)(2,1)}), bf16[1,2,256,2048]{3,2,1,0:T(8,128)(2,1)}) %all-gather.23.cloned.1.call-update) | async-done | bytes 2097168 | tf_op jit(solution)/shard_map/all_gather | solution.py:40
  401.7 91.0 %all-gather.25.cloned.1.call-done = bf16[2048,2,2048]{2,0,1:T(8,128)(2,1)} async-done(((bf16[256,2,2048]{2,0,1:T(8,128)(2,1)}), bf16[2048,2,2048]{2,0,1:T(8,128)(2,1)}) %all-gather.25.cloned.1.call-update) | async-done | bytes 16777232 | tf_op jit(solution)/shard_map/all_gather | solution.py:170
  492.7 15.1 %fusion.48 = f32[1,2,256,2,2048]{4,2,3,1,0:T(8,128)} fusion(bf16[2048,2,2048]{2,0,1:T(8,128)(2,1)} %all-gather.25.cloned.1.call-done, bf16[1,2,256,2048]{3,2,1,0:T(8,128)(2,1)} %all-gather.23.cloned.1.call-done), kind=kOutput, calls=%fused_computation.71 | convolution fusion | flops 8589934592 | bytes 27262976 | tf_op jit(solution)/shard_map/spcd,dtf->spctf/dot_general | solution.py:178
  507.8 32.2 %all-gather.29.cloned.1.call-done = bf16[1,2,256,2048]{3,2,1,0:T(8,128)(2,1)} async-done(((bf16[1,2,64,2048]{3,2,1,0:T(8,128)(2,1)}), bf16[1,2,256,2048]{3,2,1,0:T(8,128)(2,1)}) %all-gather.29.cloned.1.call-update) | async-done | bytes 2097168 | tf_op jit(solution)/shard_map/all_gather | solution.py:48
  540.0 56.4 %all-gather.27.cloned.1.call-done = bf16[2048,2048]{1,0:T(8,128)(2,1)} async-done(((bf16[2048,256]{1,0:T(8,128)(2,1)}), bf16[2048,2048]{1,0:T(8,128)(2,1)}) %all-gather.27.cloned.1.call-update) | async-done | bytes 8388624 | tf_op jit(solution)/shard_map/all_gather | solution.py:171
  596.4 11.2 fusion.71
  609.8 13.8 fusion.54
  623.6 76.9 %reduce-scatter.15.cloned.1.call-done = f32[1,2,64,2048]{3,2,1,0:T(8,128)} async-done(((f32[1,2,256,2048]{3,2,1,0:T(8,128)}), f32[1,2,64,2048]{3,2,1,0:T(8,128)}) %reduce-scatter.15.cloned.1.call-update) | async-done | bytes 1048592 | tf_op jit(solution)/shard_map/reduce_scatter | solution.py:52
  704.7 46.0 %all-gather.31.cloned.1.call-done = bf16[1,2,256,2048]{3,2,1,0:T(8,128)(2,1)} async-done(((bf16[1,2,64,2048]{3,2,1,0:T(8,128)(2,1)}), bf16[1,2,256,2048]{3,2,1,0:T(8,128)(2,1)}) %all-gather.31.cloned.1.call-update) | async-done | bytes 2097168 | tf_op jit(solution)/shard_map/all_gather | solution.py:48
  750.8 3.5 fusion.76
  760.7 122.6 %while.35 = (s32[]{:T(128)}, f32[1,512,8,64]{1,3,2,0:T(8,128)}, bf16[8,1,256,512]{3,2,0,1:T(8,128)(2,1)}, bf16[8,1,256,512]{3,2,0,1:T(8,128)(2,1)}, s32[8]{0:T(1...) while((s32[]{:T(128)}, f32[1,512,8,64]{1,3,2,0:T(8,128)}, ...), condition=%wide.wide.region_12.13_spmd.clone, body=%wide.wide.region_11.12_spmd.clone.sunk | while | flops 679871232 | bytes 27977976 | solution.py:262
  884.8 8.4 bitcast_convert_fusion.1
  894.3 4.2 bitcast_convert_fusion.3
  900.3 13.1 reduce-scatter.17.cloned.1.call-done
  927.3 20.3 %reduce-scatter.19.cloned.1.call-done = bf16[2,1,256,512]{3,2,0,1:T(8,128)(2,1)} async-done(((bf16[8,1,256,512]{3,2,0,1:T(8,128)(2,1)}), bf16[2,1,256,512]{3,2,0,1:T(8,128)(2,1)}) %reduce-scatter.19.cloned.1.call-update) | async-done | bytes 524304 | tf_op jit(solution)/shard_map/reduce_scatter | solution.py:269
  947.6 8.6 fusion.51
  957.8 11.1 fusion.57
  970.7 6.4 bitcast_convert_fusion.2
  978.7 14.6 %bitcast_convert_fusion = bf16[2048,2,2048]{2,0,1:T(8,128)(2,1)} fusion(bf16[2,256,1,2048]{3,1,0,2:T(8,128)(2,1)} %copy-done.35, bf16[2,256,1,2048]{3,1,0,2:T(8,128)(2,1)} %copy-done.34, bf16[1,2,256,2048]{3,2,1,0:T(8,128)(2,1)S(1)} %copy-done.28), kind=kOutput, calls=%fused_computation.58 | convolution fusion | flops 8606711808 | bytes 23068672 | tf_op jit(solution)/shard_map/spcd,spctf->dtf/dot_general | solution.py:197
  995.2 27.0 %reduce-scatter.29.cloned.1.call-done = bf16[2048,256]{1,0:T(8,128)(2,1)} async-done(((bf16[2048,2048]{1,0:T(8,128)(2,1)}), bf16[2048,256]{1,0:T(8,128)(2,1)}) %reduce-scatter.29.cloned.1.call-update) | async-done | bytes 1048592 | tf_op jit(solution)/shard_map/reduce_scatter | solution.py:212
  1024.9 41.6 %reduce-scatter.25.cloned.1.call-done = bf16[512,256]{1,0:T(8,128)(2,1)} async-done(((bf16[512,2048]{1,0:T(8,128)(2,1)}), bf16[512,256]{1,0:T(8,128)(2,1)}) %reduce-scatter.25.cloned.1.call-update) | async-done | bytes 262160 | tf_op jit(solution)/shard_map/reduce_scatter | solution.py:303
  1068.3 77.8 %reduce-scatter.21.cloned.1.call-done = f32[1,2,64,2048]{3,2,1,0:T(8,128)} async-done(((f32[1,2,256,2048]{3,2,1,0:T(8,128)}), f32[1,2,64,2048]{3,2,1,0:T(8,128)}) %reduce-scatter.21.cloned.1.call-update) | async-done | bytes 1048592 | tf_op jit(solution)/shard_map/reduce_scatter | solution.py:52
  1147.7 13.6 all-reduce.3
  1161.4 12.5 all-reduce.2
  1173.9 51.9 %reduce-scatter.13.cloned.1.call-done = f32[1,2,64,2048]{3,2,1,0:T(8,128)} async-done(((f32[1,2,256,2048]{3,2,1,0:T(8,128)}), f32[1,2,64,2048]{3,2,1,0:T(8,128)}) %reduce-scatter.13.cloned.1.call-update) | async-done | bytes 1048592 | tf_op jit(solution)/shard_map/reduce_scatter | solution.py:44
  1225.8 3.1 fusion.85
  1228.9 62.4 %reduce-scatter.23.cloned.1.call-done = bf16[256,3,512]{2,0,1:T(8,128)(2,1)} async-done(((bf16[2048,3,512]{2,0,1:T(8,128)(2,1)}), bf16[256,3,512]{2,0,1:T(8,128)(2,1)}) %reduce-scatter.23.cloned.1.call-update) | async-done | bytes 786448 | tf_op jit(solution)/shard_map/reduce_scatter | solution.py:300
  1293.8 117.1 %reduce-scatter.27.cloned.1.call-done = bf16[256,2,2048]{2,0,1:T(8,128)(2,1)} async-done(((bf16[2048,2,2048]{2,0,1:T(8,128)(2,1)}), bf16[256,2,2048]{2,0,1:T(8,128)(2,1)}) %reduce-scatter.27.cloned.1.call-update) | async-done | bytes 2097168 | tf_op jit(solution)/shard_map/reduce_scatter | solution.py:209
  1410.9 5.8 copy.97
  (395 shorter events, 221.6 us)
Async XLA Ops:
  7.2 50.9 %all-gather.15.cloned.1.call-start = ((), (), s32[]{:S(2)}) async-start(), calls=%async_computation.11 | async-start | bytes 7077888 | tf_op jit(solution)/shard_map/all_gather | solution.py:113
  7.9 98.0 %all-gather.13.cloned.1.call-start = ((), (), s32[]{:S(2)}) async-start(), calls=%async_computation.10 | async-start | bytes 2621440 | tf_op jit(solution)/shard_map/all_gather | solution.py:40
  19.0 1.3 copy-start.23
  20.3 0.6 copy-start.25
  23.0 126.0 %all-gather.17.cloned.1.call-start = ((), (), s32[]{:S(2)}) async-start(), calls=%async_computation.12 | async-start | bytes 2621440 | tf_op jit(solution)/shard_map/all_gather | solution.py:134
  24.3 107.7 %copy-start.11 = (f32[512,64]{0,1:T(8,128)}, f32[512,64]{0,1:T(8,128)S(1)}, u32[]{:S(2)}) copy-start(f32[512,64]{0,1:T(8,128)S(1)} %get-tuple-element.492) | copy-start | bytes 393220
  24.3 107.7 %copy-start.15 = (f32[512,64]{0,1:T(8,128)}, f32[512,64]{0,1:T(8,128)S(1)}, u32[]{:S(2)}) copy-start(f32[512,64]{0,1:T(8,128)S(1)} %get-tuple-element.491) | copy-start | bytes 393220
  26.2 40.7 %copy-start.5 = (f32[512,8,64]{0,2,1:T(8,128)}, f32[512,8,64]{0,2,1:T(8,128)S(1)}, u32[]{:S(2)}) copy-start(f32[512,8,64]{0,2,1:T(8,128)S(1)} %mul.365) | copy-start | bytes 3145732
  112.1 15.4 %copy-start.10 = (f32[1,512,3,8,64]{1,4,3,2,0:T(8,128)}, f32[1,512,3,8,64]{1,4,3,2,0:T(8,128)S(1)}, u32[]{:S(2)}) copy-start(f32[1,512,3,8,64]{1,4,3,2,0:T(8,128)S(1)} %convolution_bitcast_fusion.2) | copy-start | bytes 9437188
  127.5 46.1 %all-gather.19.cloned.1.call-start = ((), (), s32[]{:S(2)}) async-start(), calls=%async_computation.13 | async-start | bytes 2621440 | tf_op jit(solution)/shard_map/all_gather | solution.py:135
  128.4 3.6 copy-start.19
  128.4 3.6 copy-start.20
  131.1 139.3 %all-gather.21.cloned.1.call-start = ((), (), s32[]{:S(2)}) async-start(), calls=%async_computation.14 | async-start | bytes 2359296 | tf_op jit(solution)/shard_map/all_gather | solution.py:114
  131.7 221.0 %reduce-scatter.11.cloned.1.call-start = ((), (), s32[]{:S(2)}) async-start(), calls=%async_computation.15 | async-start | bytes 5242880 | tf_op jit(solution)/shard_map/reduce_scatter | solution.py:44
  152.9 24.7 %copy-start.31 = (s32[1,8]{1,0:T(1,128)S(1)}, s32[1,8]{1,0:T(1,128)}, u32[]{:S(2)}) copy-start(s32[1,8]{1,0:T(1,128)} %param.14) | copy-start | bytes 100
  183.0 3.5 copy-start
  194.6 3.4 copy-start
  206.1 3.4 copy-start
  217.7 3.4 copy-start
  229.2 3.4 copy-start
  240.8 3.4 copy-start
  252.3 3.4 copy-start
  263.9 3.4 copy-start
  270.4 5.1 copy-start.17
  275.5 0.7 copy-start.30
  275.5 77.2 %copy-start.3 = (bf16[1,2,64,2048]{3,2,1,0:T(8,128)(2,1)S(1)}, bf16[1,2,64,2048]{3,2,1,0:T(8,128)(2,1)}, u32[]{:S(2)}) copy-start(bf16[1,2,64,2048]{3,2,1,0:T(8,128)(2,1)} %param.13) | copy-start | bytes 1572868
  275.5 126.2 %all-gather.23.cloned.1.call-start = ((), (), s32[]{:S(2)}) async-start(), calls=%async_computation.16 | async-start | bytes 2621440 | tf_op jit(solution)/shard_map/all_gather | solution.py:40
  354.2 347.9 %copy-start.1 = (f32[1,2,64,2048]{3,2,1,0:T(8,128)}, f32[1,2,64,2048]{3,2,1,0:T(8,128)S(1)}, u32[]{:S(2)}) copy-start(f32[1,2,64,2048]{3,2,1,0:T(8,128)S(1)} %get-tuple-element.460) | copy-start | bytes 3145732
  355.4 137.4 %all-gather.25.cloned.1.call-start = ((), (), s32[]{:S(2)}) async-start(), calls=%async_computation.17 | async-start | bytes 18874368 | tf_op jit(solution)/shard_map/all_gather | solution.py:170
  359.2 180.8 %all-gather.29.cloned.1.call-start = ((), (), s32[]{:S(2)}) async-start(), calls=%async_computation.20 | async-start | bytes 2621440 | tf_op jit(solution)/shard_map/all_gather | solution.py:48
  360.0 236.4 %all-gather.27.cloned.1.call-start = ((), (), s32[]{:S(2)}) async-start(), calls=%async_computation.18 | async-start | bytes 9437184 | tf_op jit(solution)/shard_map/all_gather | solution.py:171
  360.6 339.9 %reduce-scatter.15.cloned.1.call-start = ((), (), s32[]{:S(2)}) async-start(), calls=%async_computation.21 | async-start | bytes 5242880 | tf_op jit(solution)/shard_map/reduce_scatter | solution.py:52
  607.7 1.3 copy-start.34
  607.7 2.1 copy-start.35
  623.5 78.6 %copy-start.8 = (bf16[1,2,64,2048]{3,2,1,0:T(8,128)(2,1)S(1)}, bf16[1,2,64,2048]{3,2,1,0:T(8,128)(2,1)}, u32[]{:S(2)}) copy-start(bf16[1,2,64,2048]{3,2,1,0:T(8,128)(2,1)} %param.21) | copy-start | bytes 1572868
  623.6 127.2 %all-gather.31.cloned.1.call-start = ((), (), s32[]{:S(2)}) async-start(), calls=%async_computation.22 | async-start | bytes 2621440 | tf_op jit(solution)/shard_map/all_gather | solution.py:48
  704.5 208.9 %reduce-scatter.17.cloned.1.call-start = ((), (), s32[]{:S(2)}) async-start(), calls=%async_computation.23 | async-start | bytes 2621440 | tf_op jit(solution)/shard_map/reduce_scatter | solution.py:266
  755.9 4.8 copy-start.13
  883.2 1.6 copy-start.29
  883.3 64.3 %reduce-scatter.19.cloned.1.call-start = ((), (), s32[]{:S(2)}) async-start(), calls=%async_computation.24 | async-start | bytes 2621440 | tf_op jit(solution)/shard_map/reduce_scatter | solution.py:269
  883.9 138.4 %reduce-scatter.29.cloned.1.call-start = ((), (), s32[]{:S(2)}) async-start(), calls=%async_computation.29 | async-start | bytes 9437184 | tf_op jit(solution)/shard_map/reduce_scatter | solution.py:212
  893.2 1.0 copy-start.18
  893.3 5.5 copy-start.6
  893.3 173.2 %reduce-scatter.25.cloned.1.call-start = ((), (), s32[]{:S(2)}) async-start(), calls=%async_computation.27 | async-start | bytes 2359296 | tf_op jit(solution)/shard_map/reduce_scatter | solution.py:303
  898.5 247.6 %reduce-scatter.21.cloned.1.call-start = ((), (), s32[]{:S(2)}) async-start(), calls=%async_computation.25 | async-start | bytes 5242880 | tf_op jit(solution)/shard_map/reduce_scatter | solution.py:52
  899.4 16.1 %copy-start.12 = (f32[512,64]{0,1:T(8,128)S(1)}, f32[512,64]{0,1:T(8,128)}, u32[]{:S(2)}) copy-start(f32[512,64]{0,1:T(8,128)} %copy-done.11) | copy-start | bytes 393220
  918.2 2.9 copy-start.16
  919.7 6.4 copy-start.14
  926.2 21.4 %copy-start.21 = (bf16[2,256,1,512]{3,1,2,0:T(8,128)(2,1)S(1)}, bf16[2,256,1,512]{3,1,2,0:T(8,128)(2,1)}, u32[]{:S(2)}) copy-start(bf16[2,256,1,512]{3,1,2,0:T(8,128)(2,1)} %copy.91) | copy-start | bytes 1572868
  956.2 1.7 copy-start.33
  956.2 269.6 %reduce-scatter.13.cloned.1.call-start = ((), (), s32[]{:S(2)}) async-start(), calls=%async_computation.19 | async-start | bytes 5242880 | tf_op jit(solution)/shard_map/reduce_scatter | solution.py:44
  969.0 1.0 copy-start.22
  969.0 1.8 copy-start.27
  969.0 322.3 %reduce-scatter.23.cloned.1.call-start = ((), (), s32[]{:S(2)}) async-start(), calls=%async_computation.26 | async-start | bytes 7077888 | tf_op jit(solution)/shard_map/reduce_scatter | solution.py:300
  977.1 1.6 copy-start.28
  977.1 433.8 %reduce-scatter.27.cloned.1.call-start = ((), (), s32[]{:S(2)}) async-start(), calls=%async_computation.28 | async-start | bytes 18874368 | tf_op jit(solution)/shard_map/reduce_scatter | solution.py:209
  993.3 0.7 copy-start.32
  993.3 152.7 %copy-start.4 = (bf16[1,2,64,2048]{3,2,1,0:T(8,128)(2,1)S(1)}, bf16[1,2,64,2048]{3,2,1,0:T(8,128)(2,1)}, u32[]{:S(2)}) copy-start(bf16[1,2,64,2048]{3,2,1,0:T(8,128)(2,1)} %param.13) | copy-start | bytes 1572868
  993.3 152.7 %copy-start.24 = (f32[8,1,256]{2,1,0:T(1,128)S(1)}, f32[8,1,256]{2,1,0:T(1,128)}, u32[]{:S(2)}) copy-start(f32[8,1,256]{2,1,0:T(1,128)} %copy-done.23) | copy-start | bytes 24580
  993.3 152.7 %copy-start.26 = (f32[2,64]{1,0:T(2,128)S(1)}, f32[2,64]{1,0:T(2,128)}, u32[]{:S(2)}) copy-start(f32[2,64]{1,0:T(2,128)} %copy-done.25) | copy-start | bytes 1540
  993.4 232.4 %copy-start.2 = (f32[1,2,64,2048]{3,2,1,0:T(8,128)S(1)}, f32[1,2,64,2048]{3,2,1,0:T(8,128)}, u32[]{:S(2)}) copy-start(f32[1,2,64,2048]{3,2,1,0:T(8,128)} %copy-done.1) | copy-start | bytes 3145732
  993.4 232.4 %copy-start.7 = (f32[1,2,64,2048]{3,2,1,0:T(8,128)S(1)}, f32[1,2,64,2048]{3,2,1,0:T(8,128)}, u32[]{:S(2)}) copy-start(f32[1,2,64,2048]{3,2,1,0:T(8,128)} %reduce-scatter.15.cloned.1.call-done) | copy-start | bytes 3145732
  993.4 232.4 %copy-start.9 = (bf16[1,2,64,2048]{3,2,1,0:T(8,128)(2,1)S(1)}, bf16[1,2,64,2048]{3,2,1,0:T(8,128)(2,1)}, u32[]{:S(2)}) copy-start(bf16[1,2,64,2048]{3,2,1,0:T(8,128)(2,1)} %param.21) | copy-start | bytes 1572868
Sparse Core Ops, SparseCore 0:
  9.9 48.1 all-gather.14
  60.2 45.6 all-gather.12
  127.6 21.3 all-gather.16
  151.0 22.5 all-gather.18
  175.3 28.0 all-gather.20
  275.6 77.0 reduce-scatter.10
  355.5 46.1 all-gather.22
  404.2 88.5 all-gather.24
  494.3 45.6 all-gather.28
  541.7 54.6 all-gather.26
  623.7 76.7 reduce-scatter.14
  704.6 46.1 all-gather.30
  883.4 29.9 reduce-scatter.16
  916.4 31.1 reduce-scatter.18
  950.9 71.2 reduce-scatter.28
  1025.3 41.1 reduce-scatter.24
  1069.2 76.7 reduce-scatter.20
  1148.2 77.5 reduce-scatter.12
  1229.2 62.0 reduce-scatter.22
  1294.7 116.1 reduce-scatter.26
where the time goes:
time: 1430 us; the launch traced here: 1420 us
  waiting for transfers between devices  931 us (65%)
  matrix products  222 us (16%)
  local copies, waits for them, and re-layouts  109 us (8%)
  other arithmetic  85.4 us (6%)
  blocking collectives  45.4 us (3%)
  between operations  16 us (1%)
    reduce_scatter x2, waiting for transfers between devices, sum_normed(): return lax.psum_scatter(values, 'tp', scatter_dimension=2, tiled=True)  155 us
    reduce_scatter x2, waiting for transfers between devices, sum_rows(): return lax.psum_scatter(values, 'tp', scatter_dimension=2, tiled=True)  119 us
    reduce_scatter x1, waiting for transfers between devices, body(): lax.psum_scatter(grad_gate_up_local.astype(jnp.bfloat16), ('dp', 'ctx'),...  117 us
    all_gather x1, waiting for transfers between devices, body(): lax.all_gather(w_gate_up, ('dp', 'ctx'), axis=0, tiled=True)  91 us
    all_gather x2, waiting for transfers between devices, gather_rows(): return lax.all_gather(values, 'tp', axis=2, tiled=True)  79.7 us
    all_gather x2, waiting for transfers between devices, gather_cotangent(): return lax.all_gather(values, 'tp', axis=2, tiled=True)  78.2 us
    reduce_scatter x1, waiting for transfers between devices, body(): lax.psum_scatter(grad_qkv_local.astype(jnp.bfloat16), ('dp', 'ctx'), scat...  62.4 us
    all_gather x1, waiting for transfers between devices, body(): lax.all_gather(w_down, ('dp', 'ctx'), axis=1, tiled=True)  56.4 us
  transfers between devices with their start and end apart: 20, of which 19 were waited for; matrix products, arithmetic and copies ran while one was open for 15% of the time, Pallas kernels for 0%

commit v1 on v0

--- a/solution.py
+++ b/solution.py
@@ -7,6 +7,24 @@
 EPSILON = 1e-05
 ROPE_BASE = 130000.0
 NEG_LARGE = -1e30
+
+
+def collect(array, axis, dim):
+    ways, here, lap = (lax.axis_size(axis), lax.axis_index(axis), array.shape[dim])
+    dims = [n * ways if d == dim else n for d, n in enumerate(array.shape)]
+    full = lax.dynamic_update_slice_in_dim(
+        jnp.zeros(dims, array.dtype), array, here * lap, axis=dim
+    )
+    going_up = going_down = array
+    for far in range(1, ways // 2 + 1):
+        going_up = lax.ppermute(going_up, axis, [(d, (d + 1) % ways) for d in range(ways)])
+        full = lax.dynamic_update_slice_in_dim(full, going_up, (here - far) % ways * lap, axis=dim)
+        if 2 * far < ways:
+            going_down = lax.ppermute(going_down, axis, [(d, (d - 1) % ways) for d in range(ways)])
+            full = lax.dynamic_update_slice_in_dim(
+                full, going_down, (here + far) % ways * lap, axis=dim
+            )
+    return full
 
 
 def rope_tables(positions, head_size):
@@ -45,7 +63,7 @@
 
 
 def gather_cotangent(values):
-    return lax.all_gather(values, "tp", axis=2, tiled=True)
+    return collect(values, "tp", 2)
 
 
 def sum_normed(values):

time: 1430 us -> 1410 us (0.986)
  waiting for transfers between devices: 931 us -> 860 us
  starting transfers between devices: 2.07 us -> 39.1 us
    all_gather x2 -> x0, waiting for transfers between devices: 78.2 us -> none  [gather_cotangent(): return lax.all_gather(values, 'tp', axis=2, tiled=True)]
    ppermute x0 -> x6, waiting for transfers between devices: none -> 61.1 us  [the longest x4 56.2 us: collect(): lax.ppermute(going_up, axis, [(d, (d + 1) % ways) for d in range(ways)])]
    all_gather x2, waiting for transfers between devices: 79.7 us -> 41.1 us  [gather_rows(): return lax.all_gather(values, 'tp', axis=2, tiled=True)]
    ppermute x0 -> x6, starting transfers between devices: none -> 37.7 us  [the longest x4 33 us: collect(): lax.ppermute(going_up, axis, [(d, (d + 1) % ways) for d in range(ways)])]
    unnamed x80 -> x88, local copies, waits for them, and re-layouts: 29.5 us -> 33.4 us
  transfers between devices with their start and end apart: 20 -> 24, of which waited for: 19 -> 23; matrix products, arithmetic and copies ran while one was open for 15% -> 16% of each run, Pallas kernels for 0% -> 0%
where the time goes in v1:
time: 1410 us; the launch traced here: 1400 us
  waiting for transfers between devices  860 us (61%)
  matrix products  220 us (16%)
  local copies, waits for them, and re-layouts  121 us (9%)
  other arithmetic  83.8 us (6%)
  blocking collectives  45.4 us (3%)
  starting transfers between devices  39.1 us (3%)
  loops' own time  17.5 us (1%)
  between operations  15.9 us (1%)
    reduce_scatter x2, waiting for transfers between devices, sum_normed(): return lax.psum_scatter(values, 'tp', scatter_dimension=2, tiled=True)  155 us
    reduce_scatter x2, waiting for transfers between devices, sum_rows(): return lax.psum_scatter(values, 'tp', scatter_dimension=2, tiled=True)  119 us
    reduce_scatter x1, waiting for transfers between devices, body(): lax.psum_scatter(grad_gate_up_local.astype(jnp.bfloat16), ('dp', 'ctx'),...  117 us
    all_gather x1, waiting for transfers between devices, body(): lax.all_gather(w_gate_up, ('dp', 'ctx'), axis=0, tiled=True)  90.4 us
    reduce_scatter x1, waiting for transfers between devices, body(): lax.psum_scatter(grad_qkv_local.astype(jnp.bfloat16), ('dp', 'ctx'), scat...  62.2 us
    ppermute x4, waiting for transfers between devices, collect(): lax.ppermute(going_up, axis, [(d, (d + 1) % ways) for d in range(ways)])  56.2 us
    all_gather x1, waiting for transfers between devices, body(): lax.all_gather(w_down, ('dp', 'ctx'), axis=1, tiled=True)  42.8 us
    reduce_scatter x1, waiting for transfers between devices, body(): lax.psum_scatter(grad_out_local.astype(jnp.bfloat16), ('dp', 'ctx'), scat...  41.6 us
  transfers between devices with their start and end apart: 24, of which 23 were waited for; matrix products, arithmetic and copies ran while one was open for 16% of the time, Pallas kernels for 0%

profile of v1, /device:TPU:0, one launch (start us, length us, event | category | flops | bytes accessed | tf_op | source)
XLA Modules:
  0.0 1402.1 jit_solution(16046635889360990156)
XLA Ops:
  8.6 10.4 all-gather
  26.6 31.4 %all-gather.13.cloned.1.call-done = bf16[2048,3,512]{2,0,1:T(8,128)(2,1)} async-done(((bf16[256,3,512]{2,0,1:T(8,128)(2,1)}), bf16[2048,3,512]{2,0,1:T(8,128)(2,1)}) %all-gather.13.cloned.1.call-update) | async-done | bytes 6291472 | tf_op jit(solution)/shard_map/all_gather | solution.py:131
  58.0 8.8 copy.74
  66.9 39.0 %all-gather.11.cloned.1.call-done = bf16[1,2,256,2048]{3,2,1,0:T(8,128)(2,1)} async-done(((bf16[1,2,64,2048]{3,2,1,0:T(8,128)(2,1)}), bf16[1,2,256,2048]{3,2,1,0:T(8,128)(2,1)}) %all-gather.11.cloned.1.call-update) | async-done | bytes 2097168 | tf_op jit(solution)/shard_map/all_gather | solution.py:58
  105.9 6.2 convolution_bitcast_fusion.2
  118.1 2.8 add_convert_fusion.1
  127.8 16.1 %all-gather.15.cloned.1.call-done = bf16[1,8,256,512]{3,2,0,1:T(8,128)(2,1)} async-done(((bf16[1,2,256,512]{3,2,0,1:T(8,128)(2,1)}), bf16[1,8,256,512]{3,2,0,1:T(8,128)(2,1)}) %all-gather.15.cloned.1.call-update) | async-done | bytes 2097168 | tf_op jit(solution)/shard_map/all_gather | solution.py:152
  143.9 3.9 copy.77
  147.8 20.7 %all-gather.17.cloned.1.call-done = bf16[1,8,256,512]{3,2,0,1:T(8,128)(2,1)} async-done(((bf16[1,2,256,512]{3,2,0,1:T(8,128)(2,1)}), bf16[1,8,256,512]{3,2,0,1:T(8,128)(2,1)}) %all-gather.17.cloned.1.call-update) | async-done | bytes 2097168 | tf_op jit(solution)/shard_map/all_gather | solution.py:153
  168.5 3.9 copy.78
  172.5 92.6 %while.34 = (s32[]{:T(128)}, f32[1,8,512]{2,1,0:T(8,128)S(1)}, f32[1,8,512]{2,1,0:T(8,128)S(1)}, f32[1,512,8,64]{1,3,2,0:T(8,128)S(1)}, s32[1,8]{1,0:T(1,128)S(1...) while((s32[]{:T(128)}, f32[1,8,512]{2,1,0:T(8,128)S(1)}, ...), condition=%wide.region_4.5_spmd.clone, body=%wide.region_1.4_spmd.clone.sunk | while | flops 947548928 | bytes 34334904 | solution.py:181
  175.0 2.8 fusion.164
  177.9 3.1 fusion.166
  186.7 2.8 fusion.164
  189.5 3.1 fusion.166
  198.2 2.8 fusion.164
  201.1 3.1 fusion.166
  209.8 2.8 fusion.164
  212.6 3.1 fusion.166
  221.4 2.8 fusion.164
  224.2 3.1 fusion.166
  232.9 2.8 fusion.164
  235.8 3.1 fusion.166
  244.5 2.8 fusion.164
  247.3 3.1 fusion.166
  256.1 2.8 fusion.164
  258.9 3.1 fusion.166
  265.4 5.1 convolution_bitcast_fusion.1
  271.2 8.9 all-gather.1
  280.1 67.6 %reduce-scatter.11.cloned.1.call-done = f32[1,2,64,2048]{3,2,1,0:T(8,128)} async-done(((f32[1,2,256,2048]{3,2,1,0:T(8,128)}), f32[1,2,64,2048]{3,2,1,0:T(8,128)}) %reduce-scatter.11.cloned.1.call-update) | async-done | bytes 1048592 | tf_op jit(solution)/shard_map/reduce_scatter | solution.py:62
  350.4 3.8 copy.80
  361.5 19.1 %collective-permute-done = bf16[1,2,64,2048]{3,2,1,0:T(8,128)(2,1)} collective-permute-done((bf16[1,2,64,2048]{3,2,1,0:T(8,128)(2,1)S(1)}, bf16[1,2,64,2048]{3,2,1,0:T(8,128)(2,1)}, u32[]{:S(2)}, u32[]{:S(2)}) %collective-permute-start) | collective-permute-done | bytes 524320 | tf_op jit(solution)/shard_map/ppermute | solution.py:20
  380.6 20.9 %collective-permute-start.2 = (bf16[1,2,64,2048]{3,2,1,0:T(8,128)(2,1)}, bf16[1,2,64,2048]{3,2,1,0:T(8,128)(2,1)S(1)}, u32[]{:S(2)}, u32[]{:S(2)}) collective-permute-start(bf16[1,2,64,2048]{3,2,1,0:T(8,128)(2,1)} %collective-permute-done), channel_id=1, source_target_pairs={{0,1},{1,2},{2,3},{3,0},{4,5},{5,6},{6,7},{7,4},{8,9},{9,10},{10,1... | collective-permute-start | bytes 1572872 | tf_op jit(solution)/shard_map/ppermute | solution.py:20
  403.5 3.8 collective-permute-done.1
  409.2 14.8 %collective-permute-done.2 = bf16[1,2,64,2048]{3,2,1,0:T(8,128)(2,1)S(1)} collective-permute-done((bf16[1,2,64,2048]{3,2,1,0:T(8,128)(2,1)}, bf16[1,2,64,2048]{3,2,1,0:T(8,128)(2,1)S(1)}, u32[]{:S(2)}, u32[]{:S(2)}) %collective-permute-start.2) | collective-permute-done | bytes 524320 | tf_op jit(solution)/shard_map/ppermute | solution.py:20
  427.0 90.4 %all-gather.23.cloned.1.call-done = bf16[2048,2,2048]{2,0,1:T(8,128)(2,1)} async-done(((bf16[256,2,2048]{2,0,1:T(8,128)(2,1)}), bf16[2048,2,2048]{2,0,1:T(8,128)(2,1)}) %all-gather.23.cloned.1.call-update) | async-done | bytes 16777232 | tf_op jit(solution)/shard_map/all_gather | solution.py:188
  517.4 15.0 %fusion.48 = f32[1,2,256,2,2048]{4,2,3,1,0:T(8,128)} fusion(bf16[2048,2,2048]{2,0,1:T(8,128)(2,1)} %all-gather.23.cloned.1.call-done, bf16[1,2,256,2048]{3,2,1,0:T(8,128)(2,1)} %all-gather.21.cloned.1.call-done), kind=kOutput, calls=%fused_computation.71 | convolution fusion | flops 8589934592 | bytes 27262976 | tf_op jit(solution)/shard_map/spcd,dtf->spctf/dot_general | solution.py:196
  532.3 42.8 %all-gather.25.cloned.1.call-done = bf16[2048,2048]{1,0:T(8,128)(2,1)} async-done(((bf16[2048,256]{1,0:T(8,128)(2,1)}), bf16[2048,2048]{1,0:T(8,128)(2,1)}) %all-gather.25.cloned.1.call-update) | async-done | bytes 8388624 | tf_op jit(solution)/shard_map/all_gather | solution.py:189
  575.2 11.3 fusion.67
  588.4 13.8 fusion.54
  602.2 76.9 %reduce-scatter.15.cloned.1.call-done = f32[1,2,64,2048]{3,2,1,0:T(8,128)} async-done(((f32[1,2,256,2048]{3,2,1,0:T(8,128)}), f32[1,2,64,2048]{3,2,1,0:T(8,128)}) %reduce-scatter.15.cloned.1.call-update) | async-done | bytes 1048592 | tf_op jit(solution)/shard_map/reduce_scatter | solution.py:70
  687.4 13.1 collective-permute-done.3
  700.5 9.1 collective-permute-start.5
  712.3 9.2 collective-permute-done.5
  722.3 2.9 fusion.72
  731.6 129.1 %while.35 = (s32[]{:T(128)}, f32[1,512,8,64]{1,3,2,0:T(8,128)}, bf16[8,1,256,512]{3,2,0,1:T(8,128)(2,1)}, bf16[8,1,256,512]{3,2,0,1:T(8,128)(2,1)}, s32[8]{0:T(1...) while((s32[]{:T(128)}, f32[1,512,8,64]{1,3,2,0:T(8,128)}, ...), condition=%wide.wide.region_12.13_spmd.clone, body=%wide.wide.region_11.12_spmd.clone.sunk | while | flops 679871232 | bytes 27977976 | solution.py:280
  862.3 8.3 bitcast_convert_fusion.1
  877.6 13.8 reduce-scatter.17.cloned.1.call-done
  894.6 2.8 broadcast_multiply_fusion.1
  908.3 17.3 %reduce-scatter.19.cloned.1.call-done = bf16[2,1,256,512]{3,2,0,1:T(8,128)(2,1)} async-done(((bf16[8,1,256,512]{3,2,0,1:T(8,128)(2,1)}), bf16[2,1,256,512]{3,2,0,1:T(8,128)(2,1)}) %reduce-scatter.19.cloned.1.call-update) | async-done | bytes 524304 | tf_op jit(solution)/shard_map/reduce_scatter | solution.py:287
  925.6 8.6 fusion.51
  935.9 11.0 fusion.57
  948.6 6.4 bitcast_convert_fusion.2
  956.7 14.6 %bitcast_convert_fusion = bf16[2048,2,2048]{2,0,1:T(8,128)(2,1)} fusion(bf16[2,256,1,2048]{3,1,0,2:T(8,128)(2,1)} %copy-done.39, bf16[2,256,1,2048]{3,1,0,2:T(8,128)(2,1)} %copy-done.38, bf16[1,2,256,2048]{3,2,1,0:T(8,128)(2,1)S(1)} %copy-done.32), kind=kOutput, calls=%fused_computation.58 | convolution fusion | flops 8606711808 | bytes 23068672 | tf_op jit(solution)/shard_map/spcd,spctf->dtf/dot_general | solution.py:215
  973.2 27.2 %reduce-scatter.29.cloned.1.call-done = bf16[2048,256]{1,0:T(8,128)(2,1)} async-done(((bf16[2048,2048]{1,0:T(8,128)(2,1)}), bf16[2048,256]{1,0:T(8,128)(2,1)}) %reduce-scatter.29.cloned.1.call-update) | async-done | bytes 1048592 | tf_op jit(solution)/shard_map/reduce_scatter | solution.py:230
  1003.1 41.6 %reduce-scatter.25.cloned.1.call-done = bf16[512,256]{1,0:T(8,128)(2,1)} async-done(((bf16[512,2048]{1,0:T(8,128)(2,1)}), bf16[512,256]{1,0:T(8,128)(2,1)}) %reduce-scatter.25.cloned.1.call-update) | async-done | bytes 262160 | tf_op jit(solution)/shard_map/reduce_scatter | solution.py:321
  1046.5 77.8 %reduce-scatter.21.cloned.1.call-done = f32[1,2,64,2048]{3,2,1,0:T(8,128)} async-done(((f32[1,2,256,2048]{3,2,1,0:T(8,128)}), f32[1,2,64,2048]{3,2,1,0:T(8,128)}) %reduce-scatter.21.cloned.1.call-update) | async-done | bytes 1048592 | tf_op jit(solution)/shard_map/reduce_scatter | solution.py:70
  1125.8 13.6 all-reduce.3
  1139.6 12.5 all-reduce.2
  1152.1 51.9 %reduce-scatter.13.cloned.1.call-done = f32[1,2,64,2048]{3,2,1,0:T(8,128)} async-done(((f32[1,2,256,2048]{3,2,1,0:T(8,128)}), f32[1,2,64,2048]{3,2,1,0:T(8,128)}) %reduce-scatter.13.cloned.1.call-update) | async-done | bytes 1048592 | tf_op jit(solution)/shard_map/reduce_scatter | solution.py:62
  1204.0 3.1 fusion.79
  1207.1 62.2 %reduce-scatter.23.cloned.1.call-done = bf16[256,3,512]{2,0,1:T(8,128)(2,1)} async-done(((bf16[2048,3,512]{2,0,1:T(8,128)(2,1)}), bf16[256,3,512]{2,0,1:T(8,128)(2,1)}) %reduce-scatter.23.cloned.1.call-update) | async-done | bytes 786448 | tf_op jit(solution)/shard_map/reduce_scatter | solution.py:318
  1271.8 117.2 %reduce-scatter.27.cloned.1.call-done = bf16[256,2,2048]{2,0,1:T(8,128)(2,1)} async-done(((bf16[2048,2,2048]{2,0,1:T(8,128)(2,1)}), bf16[256,2,2048]{2,0,1:T(8,128)(2,1)}) %reduce-scatter.27.cloned.1.call-update) | async-done | bytes 2097168 | tf_op jit(solution)/shard_map/reduce_scatter | solution.py:227
  1389.0 5.8 copy.97
  (418 shorter events, 254.2 us)
Async XLA Ops:
  7.2 15.3 %copy-start.34 = (s32[1,8]{1,0:T(1,128)S(1)}, s32[1,8]{1,0:T(1,128)}, u32[]{:S(2)}) copy-start(s32[1,8]{1,0:T(1,128)} %param.14) | copy-start | bytes 100
  7.2 50.9 %all-gather.13.cloned.1.call-start = ((), (), s32[]{:S(2)}) async-start(), calls=%async_computation.11 | async-start | bytes 7077888 | tf_op jit(solution)/shard_map/all_gather | solution.py:131
  7.9 98.0 %all-gather.11.cloned.1.call-start = ((), (), s32[]{:S(2)}) async-start(), calls=%async_computation.10 | async-start | bytes 2621440 | tf_op jit(solution)/shard_map/all_gather | solution.py:58
  19.0 3.6 copy-start.27
  20.3 2.3 copy-start.29
  22.4 121.5 %all-gather.15.cloned.1.call-start = ((), (), s32[]{:S(2)}) async-start(), calls=%async_computation.12 | async-start | bytes 2621440 | tf_op jit(solution)/shard_map/all_gather | solution.py:152
  23.0 103.2 %copy-start.13 = (f32[512,64]{0,1:T(8,128)}, f32[512,64]{0,1:T(8,128)S(1)}, u32[]{:S(2)}) copy-start(f32[512,64]{0,1:T(8,128)S(1)} %get-tuple-element.494) | copy-start | bytes 393220
  23.0 103.2 %copy-start.20 = (f32[512,64]{0,1:T(8,128)}, f32[512,64]{0,1:T(8,128)S(1)}, u32[]{:S(2)}) copy-start(f32[512,64]{0,1:T(8,128)S(1)} %get-tuple-element.493) | copy-start | bytes 393220
  24.9 41.9 %copy-start.7 = (f32[512,8,64]{0,2,1:T(8,128)}, f32[512,8,64]{0,2,1:T(8,128)S(1)}, u32[]{:S(2)}) copy-start(f32[512,8,64]{0,2,1:T(8,128)S(1)} %mul.381) | copy-start | bytes 3145732
  112.1 1.7 copy-start.11
  116.5 1.6 copy-start.12
  122.3 3.9 copy-start.24
  122.3 46.1 %all-gather.17.cloned.1.call-start = ((), (), s32[]{:S(2)}) async-start(), calls=%async_computation.13 | async-start | bytes 2621440 | tf_op jit(solution)/shard_map/all_gather | solution.py:153
  125.3 140.1 %all-gather.19.cloned.1.call-start = ((), (), s32[]{:S(2)}) async-start(), calls=%async_computation.14 | async-start | bytes 2359296 | tf_op jit(solution)/shard_map/all_gather | solution.py:132
  125.9 221.8 %reduce-scatter.11.cloned.1.call-start = ((), (), s32[]{:S(2)}) async-start(), calls=%async_computation.15 | async-start | bytes 5242880 | tf_op jit(solution)/shard_map/reduce_scatter | solution.py:62
  177.9 3.5 copy-start
  189.5 3.5 copy-start
  201.0 3.5 copy-start
  212.6 3.5 copy-start
  224.2 3.5 copy-start
  235.8 3.5 copy-start
  247.3 3.5 copy-start
  258.9 3.5 copy-start
  265.4 5.1 copy-start.22
  270.5 77.2 %copy-start.3 = (bf16[1,2,64,2048]{3,2,1,0:T(8,128)(2,1)S(1)}, bf16[1,2,64,2048]{3,2,1,0:T(8,128)(2,1)}, u32[]{:S(2)}) copy-start(bf16[1,2,64,2048]{3,2,1,0:T(8,128)(2,1)} %param.13) | copy-start | bytes 1572868
  270.5 156.4 %all-gather.21.cloned.1.call-start = ((), (), s32[]{:S(2)}) async-start(), calls=%async_computation.16 | async-start | bytes 2621440 | tf_op jit(solution)/shard_map/all_gather | solution.py:58
  349.2 331.9 %copy-start.1 = (f32[1,2,64,2048]{3,2,1,0:T(8,128)}, f32[1,2,64,2048]{3,2,1,0:T(8,128)S(1)}, u32[]{:S(2)}) copy-start(f32[1,2,64,2048]{3,2,1,0:T(8,128)S(1)} %get-tuple-element.462) | copy-start | bytes 3145732
  350.3 167.0 %all-gather.23.cloned.1.call-start = ((), (), s32[]{:S(2)}) async-start(), calls=%async_computation.17 | async-start | bytes 18874368 | tf_op jit(solution)/shard_map/all_gather | solution.py:188
  354.2 221.0 %all-gather.25.cloned.1.call-start = ((), (), s32[]{:S(2)}) async-start(), calls=%async_computation.18 | async-start | bytes 9437184 | tf_op jit(solution)/shard_map/all_gather | solution.py:189
  354.9 324.2 %reduce-scatter.15.cloned.1.call-start = ((), (), s32[]{:S(2)}) async-start(), calls=%async_computation.20 | async-start | bytes 5242880 | tf_op jit(solution)/shard_map/reduce_scatter | solution.py:70
  355.2 25.4 %collective-permute-start = (bf16[1,2,64,2048]{3,2,1,0:T(8,128)(2,1)S(1)}, bf16[1,2,64,2048]{3,2,1,0:T(8,128)(2,1)}, u32[]{:S(2)}, u32[]{:S(2)}) collective-permute-start(bf16[1,2,64,2048]{3,2,1,0:T(8,128)(2,1)S(1)} %copy-done.9), channel_id=1, source_target_pairs={{0,1},{1,2},{2,3},{3,0},{4,5},{5,6},{6,7},{7,4},{8,9},{9,10},{10,1... | collective-permute-start | bytes 1572872 | tf_op jit(solution)/shard_map/ppermute | solution.py:20
  356.7 50.6 %collective-permute-start.1 = (bf16[1,2,64,2048]{3,2,1,0:T(8,128)(2,1)S(1)}, bf16[1,2,64,2048]{3,2,1,0:T(8,128)(2,1)}, u32[]{:S(2)}, u32[]{:S(2)}) collective-permute-start(bf16[1,2,64,2048]{3,2,1,0:T(8,128)(2,1)S(1)} %copy-done.9), channel_id=1, source_target_pairs={{0,3},{1,0},{2,1},{3,2},{4,7},{5,4},{6,5},{7,6},{8,11},{9,8},{10,9... | collective-permute-start | bytes 1572872 | tf_op jit(solution)/shard_map/ppermute | solution.py:23
  380.6 43.4 %collective-permute-start.2 = (bf16[1,2,64,2048]{3,2,1,0:T(8,128)(2,1)}, bf16[1,2,64,2048]{3,2,1,0:T(8,128)(2,1)S(1)}, u32[]{:S(2)}, u32[]{:S(2)}) collective-permute-start(bf16[1,2,64,2048]{3,2,1,0:T(8,128)(2,1)} %collective-permute-done), channel_id=1, source_target_pairs={{0,1},{1,2},{2,3},{3,0},{4,5},{5,6},{6,7},{7,4},{8,9},{9,10},{10,1... | collective-permute-start | bytes 1572872 | tf_op jit(solution)/shard_map/ppermute | solution.py:20
  586.5 2.0 copy-start.39
  602.2 289.2 %reduce-scatter.17.cloned.1.call-start = ((), (), s32[]{:S(2)}) async-start(), calls=%async_computation.21 | async-start | bytes 2621440 | tf_op jit(solution)/shard_map/reduce_scatter | solution.py:284
  679.1 1.9 copy-start.5
  683.6 16.9 %collective-permute-start.3 = (bf16[1,2,64,2048]{3,2,1,0:T(8,128)(2,1)}, bf16[1,2,64,2048]{3,2,1,0:T(8,128)(2,1)S(1)}, u32[]{:S(2)}, u32[]{:S(2)}) collective-permute-start(bf16[1,2,64,2048]{3,2,1,0:T(8,128)(2,1)} %get-tuple-element.460), channel_id=1, source_target_pairs={{0,1},{1,2},{2,3},{3,0},{4,5},{5,6},{6,7},{7,4},{8,9},{9,10},{10,1... | collective-permute-start | bytes 1572872 | tf_op jit(solution)/shard_map/ppermute | solution.py:20
  685.1 37.2 %copy-start.17 = (bf16[512,2048]{1,0:T(8,128)(2,1)S(1)}, bf16[512,2048]{1,0:T(8,128)(2,1)}, u32[]{:S(2)}) copy-start(bf16[512,2048]{1,0:T(8,128)(2,1)} %all-gather.19.cloned.1.call-done) | copy-start | bytes 6291460
  685.1 26.4 %collective-permute-start.4 = (bf16[1,2,64,2048]{3,2,1,0:T(8,128)(2,1)}, bf16[1,2,64,2048]{3,2,1,0:T(8,128)(2,1)S(1)}, u32[]{:S(2)}, u32[]{:S(2)}) collective-permute-start(bf16[1,2,64,2048]{3,2,1,0:T(8,128)(2,1)} %get-tuple-element.460), channel_id=1, source_target_pairs={{0,3},{1,0},{2,1},{3,2},{4,7},{5,4},{6,5},{7,6},{8,11},{9,8},{10,9... | collective-permute-start | bytes 1572872 | tf_op jit(solution)/shard_map/ppermute | solution.py:23
  700.5 21.0 %collective-permute-start.5 = (bf16[1,2,64,2048]{3,2,1,0:T(8,128)(2,1)S(1)}, bf16[1,2,64,2048]{3,2,1,0:T(8,128)(2,1)S(1)}, u32[]{:S(2)}, u32[]{:S(2)}) collective-permute-start(bf16[1,2,64,2048]{3,2,1,0:T(8,128)(2,1)S(1)} %collective-permute-done.3), channel_id=1, source_target_pairs={{0,1},{1,2},{2,3},{3,0},{4,5},{5,6},{6,7},{7,4},{8,9},{9,10},{10,1... | collective-permute-start | bytes 1572872 | tf_op jit(solution)/shard_map/ppermute | solution.py:20
  726.8 2.6 copy-start.18
  860.7 1.6 copy-start.36
  860.7 64.9 %reduce-scatter.19.cloned.1.call-start = ((), (), s32[]{:S(2)}) async-start(), calls=%async_computation.22 | async-start | bytes 2621440 | tf_op jit(solution)/shard_map/reduce_scatter | solution.py:287
  861.3 139.1 %reduce-scatter.29.cloned.1.call-start = ((), (), s32[]{:S(2)}) async-start(), calls=%async_computation.27 | async-start | bytes 9437184 | tf_op jit(solution)/shard_map/reduce_scatter | solution.py:230
  870.6 1.6 copy-start.16
  870.6 1.7 copy-start.23
  870.6 174.0 %reduce-scatter.25.cloned.1.call-start = ((), (), s32[]{:S(2)}) async-start(), calls=%async_computation.25 | async-start | bytes 2359296 | tf_op jit(solution)/shard_map/reduce_scatter | solution.py:321
  874.9 249.3 %reduce-scatter.21.cloned.1.call-start = ((), (), s32[]{:S(2)}) async-start(), calls=%async_computation.23 | async-start | bytes 5242880 | tf_op jit(solution)/shard_map/reduce_scatter | solution.py:70
  877.6 16.9 %copy-start.14 = (f32[512,64]{0,1:T(8,128)S(1)}, f32[512,64]{0,1:T(8,128)}, u32[]{:S(2)}) copy-start(f32[512,64]{0,1:T(8,128)} %copy-done.13) | copy-start | bytes 393220
  899.2 3.0 copy-start.21
  902.2 5.0 copy-start.19
  907.2 18.4 %copy-start.25 = (bf16[2,256,1,512]{3,1,2,0:T(8,128)(2,1)S(1)}, bf16[2,256,1,512]{3,1,2,0:T(8,128)(2,1)}, u32[]{:S(2)}) copy-start(bf16[2,256,1,512]{3,1,2,0:T(8,128)(2,1)} %copy.91) | copy-start | bytes 1572868
  934.2 1.7 copy-start.37
  934.2 269.8 %reduce-scatter.13.cloned.1.call-start = ((), (), s32[]{:S(2)}) async-start(), calls=%async_computation.19 | async-start | bytes 5242880 | tf_op jit(solution)/shard_map/reduce_scatter | solution.py:62
  946.9 1.8 copy-start.31
  946.9 322.4 %reduce-scatter.23.cloned.1.call-start = ((), (), s32[]{:S(2)}) async-start(), calls=%async_computation.24 | async-start | bytes 7077888 | tf_op jit(solution)/shard_map/reduce_scatter | solution.py:318
  955.1 1.6 copy-start.32
  955.1 433.9 %reduce-scatter.27.cloned.1.call-start = ((), (), s32[]{:S(2)}) async-start(), calls=%async_computation.26 | async-start | bytes 18874368 | tf_op jit(solution)/shard_map/reduce_scatter | solution.py:227
  971.3 152.9 %copy-start.4 = (bf16[1,2,64,2048]{3,2,1,0:T(8,128)(2,1)S(1)}, bf16[1,2,64,2048]{3,2,1,0:T(8,128)(2,1)}, u32[]{:S(2)}) copy-start(bf16[1,2,64,2048]{3,2,1,0:T(8,128)(2,1)} %param.13) | copy-start | bytes 1572868
  971.3 152.9 %copy-start.28 = (f32[8,1,256]{2,1,0:T(1,128)S(1)}, f32[8,1,256]{2,1,0:T(1,128)}, u32[]{:S(2)}) copy-start(f32[8,1,256]{2,1,0:T(1,128)} %copy-done.27) | copy-start | bytes 24580
  971.3 152.9 %copy-start.30 = (f32[2,64]{1,0:T(2,128)S(1)}, f32[2,64]{1,0:T(2,128)}, u32[]{:S(2)}) copy-start(f32[2,64]{1,0:T(2,128)} %copy-done.29) | copy-start | bytes 1540
  973.1 230.8 %copy-start.2 = (f32[1,2,64,2048]{3,2,1,0:T(8,128)S(1)}, f32[1,2,64,2048]{3,2,1,0:T(8,128)}, u32[]{:S(2)}) copy-start(f32[1,2,64,2048]{3,2,1,0:T(8,128)} %copy-done.1) | copy-start | bytes 3145732
  973.2 230.8 %copy-start.6 = (f32[1,2,64,2048]{3,2,1,0:T(8,128)S(1)}, f32[1,2,64,2048]{3,2,1,0:T(8,128)}, u32[]{:S(2)}) copy-start(f32[1,2,64,2048]{3,2,1,0:T(8,128)} %reduce-scatter.15.cloned.1.call-done) | copy-start | bytes 3145732
  973.2 230.8 %copy-start.10 = (bf16[1,2,64,2048]{3,2,1,0:T(8,128)(2,1)S(1)}, bf16[1,2,64,2048]{3,2,1,0:T(8,128)(2,1)}, u32[]{:S(2)}) copy-start(bf16[1,2,64,2048]{3,2,1,0:T(8,128)(2,1)} %param.21) | copy-start | bytes 1572868
  (7 other events, 7.3 us)
Sparse Core Ops, SparseCore 0:
  9.9 48.1 all-gather.12
  60.2 45.6 all-gather.10
  122.5 21.3 all-gather.14
  145.9 22.5 all-gather.16
  170.2 28.0 all-gather.18
  270.6 77.0 reduce-scatter.10
  350.5 76.4 all-gather.20
  429.4 87.9 all-gather.22
  519.3 55.8 all-gather.24
  602.3 76.7 reduce-scatter.14
  860.8 30.5 reduce-scatter.16
  894.4 31.1 reduce-scatter.18
  929.0 71.2 reduce-scatter.28
  1003.5 41.1 reduce-scatter.24
  1047.4 76.7 reduce-scatter.20
  1126.4 77.5 reduce-scatter.12
  1207.2 62.0 reduce-scatter.22
  1272.7 116.1 reduce-scatter.26
